TPU v7x, 512 devices: a whole 4x8x8 slice. The times are simulated.
512 devices in a mesh: head: 8 (over z_hi, core), vis: 64 (over y, x, z_lo).
Axes of the slice: x: 4, y: 8, z: 8 (z_hi: 4, z_lo: 2; z = z_hi * 2 + z_lo), core: 2. Of those that a mesh axis runs over, the one named last changes fastest.
Arguments:
- queries: bfloat16 [2, 512, 4096], P(None, 'vis', 'head'), may hold values from -24 to 24
- keys: bfloat16 [2, 25600, 1024], P(None, 'vis', 'head'), may hold values from -24 to 24
- values: bfloat16 [2, 25600, 1024], P(None, 'vis', 'head'), may hold values from -6 to 6
- d_out: bfloat16 [2, 512, 4096], P(None, 'vis', 'head'), may hold values from -6 to 6
- q_weight: bfloat16 [4096, 4096], P('vis', 'head'), may hold values from -0.09375 to 0.09375
Outputs:
- d_input: bfloat16 [2, 512, 4096], P(None, 'head', 'vis')
- d_keys: bfloat16 [2, 25600, 1024], P(None, 'vis', 'head')
- d_values: bfloat16 [2, 25600, 1024], P(None, 'vis', 'head')
All inputs are finite; a program needn't handle non-finite values.
Results may differ from a plain program's by a relative error of at most 0.014.
Values may be sent and summed in bfloat16 or wider, within the bound.
No kernel may reach another device: no remote copies, remote signals or barrier semaphores. Data moves between devices by JAX's collectives and lax.ppermute only.
A program may use at most 64 MiB of HBM per device.

v0:
```python
import math

import jax
import jax.numpy as jnp
from jax import lax
from jax.sharding import Mesh
from jax.sharding import PartitionSpec as P

HQ = 32
KVH = 8
HD = 128
VIS = ("vis_0", "vis_1", "vis_2")


def in_one_piece(arrays, axis, dim, along):
    both = jnp.concatenate(arrays, axis=along)
    whole, at, outs = (lax.all_gather(both, axis, axis=dim, tiled=True), 0, [])
    for a in arrays:
        outs.append(lax.slice_in_dim(whole, at, at + a.shape[along], axis=along))
        at += a.shape[along]
    return tuple(outs)


def gathered_once(array, axis):
    leaves = jax.tree.leaves(array)
    order = sorted(range(len(leaves)), key=lambda k: -leaves[k].size)
    width = (1, *leaves[order[0]].shape)[-1]
    lines = [
        jnp.pad(leaves[k].reshape(-1), (0, -leaves[k].size % width)).reshape(-1, width)
        for k in order
    ]
    both, at, found = (lax.all_gather(jnp.concatenate(lines), axis), 0, {})
    for k, line in zip(order, lines):
        piece = both[:, at : at + len(line)].reshape(len(both), -1)
        found[k] = piece[:, : leaves[k].size].reshape(-1, *leaves[k].shape)
        at += len(line)
    numbers = iter(range(len(leaves)))
    return jax.tree.map(lambda _: found[next(numbers)], array)


def combined_by_axis(array, axes, combine):
    for axis in axes:
        pieces = gathered_once(array, axis)
        array = jax.tree.map(lambda part: part[0], pieces)
        for k in range(1, lax.axis_size(axis)):
            array = combine(array, jax.tree.map(lambda part: part[k], pieces))
    return array


def cut_along(array, dim, devices):
    before, after = (array.shape[:dim], array.shape[dim + 1 :])
    return jnp.moveaxis(array.reshape(*before, devices, -1, *after), dim, 0)


def sent_and_summed(array, axis, dim):
    pieces = cut_along(array, dim, lax.axis_size(axis))
    arrived = lax.all_to_all(pieces, axis, split_axis=0, concat_axis=0, tiled=True)
    return arrived.sum(axis=0)


def from_everyone(array, axis):
    copies = jnp.broadcast_to(array, (lax.axis_size(axis), *array.shape))
    return lax.all_to_all(copies, axis, split_axis=0, concat_axis=0, tiled=True)


def laid_out(pieces, dim):
    lengths = list(pieces.shape[1:])
    lengths[dim] *= pieces.shape[0]
    return jnp.moveaxis(pieces, 0, dim).reshape(lengths)


def gathered_copies(array, axis, dim):
    pieces = from_everyone(array, axis)
    return laid_out(pieces, dim)


def summed_on_arrival(array, axis, dim):
    pieces = cut_along(array, dim, lax.axis_size(axis))
    arrived = lax.all_to_all(pieces, axis, split_axis=0, concat_axis=0, tiled=True)
    return arrived.astype(jnp.float32).sum(axis=0)


def split_query(block):
    return block.reshape(block.shape[0], block.shape[1], -1, HQ // KVH, HD)


def split_key(block):
    return block.reshape(block.shape[0], block.shape[1], -1, HD)


def block_scores(query_block, key_block):
    product = jnp.einsum(
        "brkgd,bjkd->bkgrj",
        split_query(query_block),
        split_key(key_block),
        preferred_element_type=jnp.float32,
    )
    return product * HD ** (-0.5)


def grad_products(grad_block, value_block):
    return jnp.einsum(
        "brkgd,bjkd->bkgrj",
        split_query(grad_block),
        split_key(value_block),
        preferred_element_type=jnp.float32,
    )


def local_stats(query_block, grad_block, keys, values):
    scores = block_scores(query_block, keys)
    run_peak = jnp.max(scores, axis=-1)
    weights_exp = jnp.exp(scores - run_peak[..., None])
    run_total = jnp.sum(weights_exp, axis=-1)
    grad_probs = grad_products(grad_block, values)
    run_weighted = jnp.sum(weights_exp * grad_probs, axis=-1)
    return (run_peak, run_total, run_weighted)


def combine_stats(first, second):
    peak_new = jnp.maximum(first[0], second[0])
    scale_first = jnp.exp(first[0] - peak_new)
    scale_second = jnp.exp(second[0] - peak_new)
    total_new = first[1] * scale_first + second[1] * scale_second
    weighted_new = first[2] * scale_first + second[2] * scale_second
    return (peak_new, total_new, weighted_new)


def local_grads(query_block, grad_block, log_part, delta_part, keys, values):
    inv_root = HD ** (-0.5)
    scores = block_scores(query_block, keys)
    probs = jnp.exp(scores - log_part[..., None])
    probs_low = probs.astype(jnp.bfloat16)
    grad_probs = grad_products(grad_block, values)
    grad_low = (probs * (grad_probs - delta_part[..., None])).astype(jnp.bfloat16)
    query_split = split_query(query_block)
    grad_split = split_query(grad_block)
    key_split = split_key(keys)
    batch_size, row_count, query_width = query_block.shape
    batch_size, vis_rows, key_width = keys.shape
    dq_add = (
        jnp.einsum("bkgrj,bjkd->brkgd", grad_low, key_split, preferred_element_type=jnp.float32)
        * inv_root
    )
    key_add = (
        jnp.einsum("bkgrj,brkgd->bjkd", grad_low, query_split, preferred_element_type=jnp.float32)
        * inv_root
    )
    value_add = jnp.einsum(
        "bkgrj,brkgd->bjkd", probs_low, grad_split, preferred_element_type=jnp.float32
    )
    return (
        dq_add.reshape(batch_size, row_count, query_width),
        key_add.reshape(batch_size, vis_rows, key_width),
        value_add.reshape(batch_size, vis_rows, key_width),
    )


def per_device(queries, keys, values, d_out, q_weight):
    batch_size, row_count, query_width = queries.shape
    kv_local = keys.shape[2] // HD
    groups = HQ // KVH
    key_zero = jnp.zeros(keys.shape, jnp.float32)
    whole_query, whole_grad = in_one_piece((queries, d_out), VIS, 1, 0)
    text_len = whole_query.shape[1]
    block_rows = math.gcd(text_len, 128)
    block_count = text_len // block_rows
    whole_shape = (batch_size, kv_local, groups, text_len)

    def gather_stats(step_index, acc):
        start = step_index * block_rows
        query_block = lax.dynamic_slice_in_dim(whole_query, start, block_rows, 1)
        grad_block = lax.dynamic_slice_in_dim(whole_grad, start, block_rows, 1)
        parts = local_stats(query_block, grad_block, keys, values)
        return tuple(
            (
                lax.dynamic_update_slice_in_dim(held, piece, start, 3)
                for held, piece in zip(acc, parts)
            )
        )

    blank = jnp.zeros(whole_shape, jnp.float32)
    local_all = lax.fori_loop(0, block_count, gather_stats, (blank, blank, blank))
    run_peak, run_total, run_weighted = combined_by_axis(local_all, VIS, combine_stats)
    log_total = run_peak + jnp.log(run_total)
    delta_sum = run_weighted / run_total

    def gather_grads(step_index, acc):
        dq_all, key_acc, value_acc = acc
        start = step_index * block_rows
        query_block = lax.dynamic_slice_in_dim(whole_query, start, block_rows, 1)
        grad_block = lax.dynamic_slice_in_dim(whole_grad, start, block_rows, 1)
        log_block = lax.dynamic_slice_in_dim(log_total, start, block_rows, 3)
        delta_block = lax.dynamic_slice_in_dim(delta_sum, start, block_rows, 3)
        dq_add, key_add, value_add = local_grads(
            query_block, grad_block, log_block, delta_block, keys, values
        )
        dq_all = lax.dynamic_update_slice_in_dim(dq_all, dq_add, start, 1)
        return (dq_all, key_acc + key_add, value_acc + value_add)

    dq_start = jnp.zeros(whole_query.shape, jnp.float32)
    dq_all, key_acc, value_acc = lax.fori_loop(
        0, block_count, gather_grads, (dq_start, key_zero, key_zero)
    )
    dq_home = sent_and_summed(dq_all, VIS, 1)
    dq_low = dq_home.astype(jnp.bfloat16)
    partial_input = jnp.einsum(
        "btq,dq->btd", gathered_copies(dq_low, VIS, 1), q_weight, preferred_element_type=jnp.float32
    )
    d_input = summed_on_arrival(partial_input.astype(jnp.bfloat16), "head", 1).astype(jnp.bfloat16)
    return (d_input, key_acc.astype(jnp.bfloat16), value_acc.astype(jnp.bfloat16))


def solution(mesh):
    torus = Mesh(
        mesh.devices.reshape(mesh.shape["head"], 8, 4, 2), ("head", "vis_0", "vis_1", "vis_2")
    )
    return jax.shard_map(
        per_device,
        mesh=torus,
        in_specs=(
            P(None, VIS, "head"),
            P(None, VIS, "head"),
            P(None, VIS, "head"),
            P(None, VIS, "head"),
            P(VIS, "head"),
        ),
        out_specs=(P(None, "head", VIS), P(None, VIS, "head"), P(None, VIS, "head")),
        check_vma=False,
    )
```

profile of v0, /device:TPU:1, one launch (start us, length us, event | category | flops | bytes accessed | tf_op | source)
XLA Modules:
  0.0 489.8 jit_solution(7255462232542603374)
XLA Ops:
  8.7 262.8 %all-gather.5.cloned.1.call-done = bf16[4,512,512]{2,0,1:T(4,128)(2,1)} async-done(((bf16[4,8,512]{2,0,1:T(4,128)(2,1)}), bf16[4,512,512]{2,0,1:T(4,128)(2,1)}) %all-gather.5.cloned.1.call-update) | async-done | bytes 2097168 | tf_op jit(solution)/shard_map/all_gather | solution.py:17
  271.4 4.8 fusion.95
  276.2 2.5 copy.31
  278.7 2.5 copy.32
  281.3 8.7 %while.35 = (s32[]{:T(128)}, f32[2,1,4,512]{3,2,0,1:T(4,128)S(1)}, f32[2,1,4,512]{3,2,1,0:T(4,128)S(1)}, f32[2,1,4,512]{3,2,1,0:T(4,128)S(1)}, bf16[2,512,512]{1...) while((s32[]{:T(128)}, f32[2,1,4,512]{3,2,0,1:T(4,128)S(1)}, ...), condition=%wide.region_4.0_spmd, body=%wide.region_0.0_spmd.sunk | while | flops 213398528 | bytes 6942899 | solution.py:183
  281.3 1.0 constant_dynamic-slice_fusion.7
  283.5 1.0 constant_dynamic-slice_fusion.7
  285.7 1.0 constant_dynamic-slice_fusion.7
  287.9 1.0 constant_dynamic-slice_fusion.7
  290.1 20.7 %all-gather = f32[192,512]{1,0:T(8,128)S(1)} all-gather(f32[24,512]{1,0:T(8,128)S(1)} %pad_maximum_fusion), channel_id=2, replica_groups=mesh['head'=8,'vis_0'=8,'vis_1'=4,'vis_2'=2] {'vis_0'}, dimensions={0}, use_global_device_ids=true | all-gather | bytes 442368 | tf_op jit(solution)/shard_map/all_gather | solution.py:32
  310.8 9.7 %all-gather.1 = f32[96,512]{1,0:T(8,128)S(1)} all-gather(f32[24,512]{1,0:T(8,128)S(1)} %pad_maximum_fusion.1), channel_id=3, replica_groups=mesh['head'=8,'vis_0'=8,'vis_1'=4,'vis_2'=2] {'vis_1'}, dimensions={0}, use_global_device_ids=true | all-gather | bytes 245760 | tf_op jit(solution)/shard_map/all_gather | solution.py:32
  320.6 3.6 all-gather.2
  324.3 1.6 broadcast_in_dim.21.clone
  325.9 16.2 %while.36 = (s32[]{:T(128)}, f32[2,512,512]{2,1,0:T(8,128)}, f32[2,400,128]{2,1,0:T(8,128)S(1)}, f32[2,400,128]{2,1,0:T(8,128)S(1)}, bf16[2,512,512]{1,2,0:T(8,1...) while((s32[]{:T(128)}, f32[2,512,512]{2,1,0:T(8,128)}, ...), condition=%wide.region_6.7_spmd.clone, body=%wide.region_5.6_spmd.clone.sunk | while | flops 527388672 | bytes 14368978 | solution.py:202
  325.9 1.0 constant_dynamic-slice_fusion.9
  330.0 1.0 constant_dynamic-slice_fusion.9
  334.0 1.0 constant_dynamic-slice_fusion.9
  338.1 1.0 constant_dynamic-slice_fusion.9
  342.1 1.8 copy.35
  343.9 35.0 %all_to_all.15 = f32[64,2,8,512]{3,2,1,0:T(8,128)S(1)} all-to-all(f32[64,2,8,512]{3,2,1,0:T(8,128)S(1)} %copy.35), channel_id=1, replica_groups=mesh['head'=8,'vis_0'=8,'vis_1'=4,'vis_2'=2] {'vis_0','vis_1','vis_2'}, dimensions={0} | all-to-all | bytes 4194304 | tf_op jit(solution)/shard_map/all_to_all | solution.py:57
  379.2 24.0 %all_to_all.16 = bf16[64,2,8,512]{3,2,1,0:T(8,128)(2,1)S(1)} all-to-all(bf16[64,2,8,512]{3,2,1,0:T(8,128)(2,1)S(1)} %broadcast_in_dim.24), channel_id=1, replica_groups=mesh['head'=8,'vis_0'=8,'vis_1'=4,'vis_2'=2] {'vis_0','vis_1','vis_2'}, dimensions={0} | all-to-all | bytes 2097152 | tf_op jit(solution)/shard_map/all_to_all | solution.py:63
  403.9 0.9 reshape.780
  404.8 69.2 %all-to-all-start.2 = ((bf16[8,2,4096]{2,1,0:T(2,128)(2,1)}), bf16[8,2,4096]{2,1,0:T(2,128)(2,1)S(1)}, u32[]{:S(2)}, u32[]{:S(2)}) async-start(bf16[8,2,4096]{2,1,0:T(2,128)(2,1)} %reshape.780), calls=%async_computation.2 | async-start | bytes 262144 | tf_op jit(solution)/shard_map/all_to_all | solution.py:79
  475.4 6.6 %all-to-all-done.2 = bf16[8,2,4096]{2,1,0:T(2,128)(2,1)S(1)} async-done(((bf16[8,2,4096]{2,1,0:T(2,128)(2,1)}), bf16[8,2,4096]{2,1,0:T(2,128)(2,1)S(1)}, u32[]{:S(2)}, u32[]{:S(2)}) %all-to-all-start.2) | async-done | bytes 131104 | tf_op jit(solution)/shard_map/all_to_all | solution.py:79
  (99 shorter events, 21.7 us)
Async XLA Ops:
  7.2 396.0 %copy-start = (bf16[64,512]{1,0:T(8,128)(2,1)S(1)}, bf16[64,512]{1,0:T(8,128)(2,1)}, u32[]{:S(2)}) copy-start(bf16[64,512]{1,0:T(8,128)(2,1)} %param.13) | copy-start | bytes 196612
  7.2 264.3 %all-gather.5.cloned.1.call-start = ((), (), s32[]{:S(2)}) async-start(), calls=%async_computation.3 | async-start | bytes 2129920 | tf_op jit(solution)/shard_map/all_gather | solution.py:17
  276.2 5.0 %copy-start.1 = (bf16[2,400,128]{2,1,0:T(8,128)(2,1)S(1)}, bf16[2,400,128]{2,1,0:T(8,128)(2,1)}, u32[]{:S(2)}) copy-start(bf16[2,400,128]{2,1,0:T(8,128)(2,1)} %param.10) | copy-start | bytes 614404
  276.2 5.0 %copy-start.2 = (bf16[2,400,128]{2,1,0:T(8,128)(2,1)S(1)}, bf16[2,400,128]{2,1,0:T(8,128)(2,1)}, u32[]{:S(2)}) copy-start(bf16[2,400,128]{2,1,0:T(8,128)(2,1)} %param.11) | copy-start | bytes 614404
  404.8 77.2 %all-to-all-start.2 = ((bf16[8,2,4096]{2,1,0:T(2,128)(2,1)}), bf16[8,2,4096]{2,1,0:T(2,128)(2,1)S(1)}, u32[]{:S(2)}, u32[]{:S(2)}) async-start(bf16[8,2,4096]{2,1,0:T(2,128)(2,1)} %reshape.780), calls=%async_computation.2 | async-start | bytes 262144 | tf_op jit(solution)/shard_map/all_to_all | solution.py:79
Sparse Core Ops, SparseCore 0:
  10.6 260.7 all-gather.4
where the time goes:
time: 490 us
  waiting for transfers between devices  269 us (55%)
  blocking collectives  92.9 us (19%)
  starting transfers between devices  69.2 us (14%)
  local copies, waits for them, and re-layouts  28.5 us (6%)
  between operations  14.2 us (3%)
  matrix products  11.5 us (2%)
    all_gather x1, waiting for transfers between devices, in_one_piece(): whole, at, outs = (lax.all_gather(both, axis, axis=dim, tiled=True), 0, [])  263 us
    all_to_all x1, starting transfers between devices, summed_on_arrival(): lax.all_to_all(pieces, axis, split_axis=0, concat_axis=0, tiled=True)  69.2 us
    all_to_all x1, blocking collectives, sent_and_summed(): lax.all_to_all(pieces, axis, split_axis=0, concat_axis=0, tiled=True)  35 us
    all_gather x3, blocking collectives, gathered_once(): both, at, found = (lax.all_gather(jnp.concatenate(lines), axis), 0, {})  33.9 us
    all_to_all x1, blocking collectives, from_everyone(): return lax.all_to_all(copies, axis, split_axis=0, concat_axis=0, tiled=True)  24 us
  transfers between devices with their start and end apart: 2, of which 2 were waited for; matrix products, arithmetic and copies ran while one was open for 0% of the time, Pallas kernels for 0%

commit v1 on v0

v1 whole, which is shorter than its diff:
```python
import jax
import jax.numpy as jnp
from jax import lax
from jax.sharding import Mesh
from jax.sharding import PartitionSpec as P

HQ = 32
KVH = 8
HD = 128
GROUPS = HQ // KVH
VIS = ("vis_0", "vis_1", "vis_2")
PAIR = "vis_2"
SCALE = HD ** (-0.5)
BF16 = jnp.bfloat16
F32 = jnp.float32


def exchanged(pieces, axes):
    return lax.all_to_all(pieces, axes, split_axis=0, concat_axis=0, tiled=True)


def swapped(array):
    return lax.ppermute(array, PAIR, [(0, 1), (1, 0)])


def rounded(array):
    return lax.reduce_precision(array, exponent_bits=8, mantissa_bits=7)


def in_pieces(array, count):
    out = []
    for _ in range(count):
        piece = rounded(array)
        out.append(piece.astype(BF16))
        array = array - piece
    return out


def whole_again(pieces):
    total = pieces[-1].astype(F32)
    for piece in reversed(pieces[:-1]):
        total = total + piece.astype(F32)
    return total


def first_pass(query, grad, keys, values):
    scores = jnp.einsum("jd,tgd->gjt", keys, query, preferred_element_type=F32) * SCALE
    peak = rounded(jnp.max(scores, axis=1))
    weights = jnp.exp(scores - peak[:, None])
    grad_probs = jnp.einsum("jd,tgd->gjt", values, grad, preferred_element_type=F32)
    total = jnp.sum(weights, axis=1)
    mean = jnp.sum(weights * grad_probs, axis=1) / total
    low = weights.astype(BF16)
    centred = (weights * (grad_probs - mean[:, None])).astype(BF16)
    term_a = jnp.einsum("gjt,jd->tgd", centred, keys, preferred_element_type=F32)
    term_b = jnp.einsum("gjt,jd->tgd", low, keys, preferred_element_type=F32)
    return peak, total, mean, low, centred, term_a.astype(BF16), term_b.astype(BF16)


def second_pass(low, centred, query, grad, scale, shift):
    by_row = scale.T[..., None]
    grad_scaled = (grad.astype(F32) * by_row).astype(BF16)
    query_scaled = (query.astype(F32) * by_row).astype(BF16)
    query_shifted = (query.astype(F32) * (by_row * shift.T[..., None])).astype(BF16)
    d_values = jnp.einsum("gjt,tgd->jd", low, grad_scaled, preferred_element_type=F32)
    d_keys = jnp.einsum("gjt,tgd->jd", centred, query_scaled, preferred_element_type=F32)
    d_keys = d_keys + jnp.einsum("gjt,tgd->jd", low, query_shifted, preferred_element_type=F32)
    return (d_keys * SCALE).astype(BF16), d_values.astype(BF16)


def per_device(queries, keys, values, d_out, q_weight):
    batch, rows, width = queries.shape
    shards = lax.axis_size(VIS)
    half = shards // batch
    heads = lax.axis_size("head")
    text = rows * shards
    lines = rows * GROUPS
    mine = lax.axis_index(PAIR)

    def pick(array, which):
        return jnp.where(which == 0, array[0], array[1])

    def in_order(own, other):
        return jnp.where(mine == 0, jnp.stack([own, other]), jnp.stack([other, own]))

    both = jnp.stack([keys, values])
    own_kv = jnp.where(mine == 0, both[:, 0], both[:, 1])
    other_kv = swapped(jnp.where(mine == 0, both[:, 1], both[:, 0]))
    kv = jnp.concatenate([own_kv, other_kv], axis=1)
    weight = in_order(q_weight, swapped(q_weight))

    sent = jnp.stack([queries, d_out], axis=1)
    sent = jnp.broadcast_to(sent, (half, *sent.shape)).reshape(shards, 2, rows, width)
    whole = exchanged(sent, VIS)
    query = whole[:, 0].reshape(text, GROUPS, HD)
    grad = whole[:, 1].reshape(text, GROUPS, HD)

    peak, total, mean, low, centred, term_a, term_b = first_pass(query, grad, kv[0], kv[1])

    def stat_lines(pieces):
        packed = jnp.stack([p.reshape(GROUPS, shards, rows) for p in pieces])
        packed = packed.transpose(2, 0, 3, 1).reshape(shards, -1)
        packed = jnp.pad(packed, ((0, 0), (0, -packed.shape[1] % HD)))
        return packed.reshape(shards, -1, HD)

    stats = stat_lines(in_pieces(peak, 1) + in_pieces(total, 2) + in_pieces(mean, 3))
    terms = [term_a.reshape(shards, lines, HD), term_b.reshape(shards, lines, HD), stats]
    home = exchanged(jnp.concatenate(terms, axis=1), VIS)
    home = home.reshape(half, batch, -1, HD)
    home_a = home[:, :, :lines].astype(F32)
    home_b = home[:, :, lines : 2 * lines].astype(F32)
    home_stats = home[:, :, 2 * lines :].reshape(half, batch, -1)[:, :, : 6 * lines]
    home_stats = home_stats.reshape(half, batch, 6, lines)
    peaks = home_stats[:, :, 0].astype(F32)
    totals = whole_again([home_stats[:, :, k] for k in (1, 2)])
    means = whole_again([home_stats[:, :, k] for k in (3, 4, 5)])
    peak_all = jnp.max(peaks, axis=0)
    share = jnp.exp(peaks - peak_all) * totals
    total_all = jnp.sum(share, axis=0)
    delta = jnp.sum(share * means, axis=0) / total_all
    factor = jnp.exp(peaks - peak_all) / total_all
    dq = jnp.sum(factor[..., None] * home_a + (factor * (means - delta))[..., None] * home_b, axis=0)
    dq_low = (dq * SCALE).astype(BF16)
    log_total = peak_all + jnp.log(total_all)

    back = jnp.stack(in_pieces(log_total, 3) + in_pieces(delta, 3), axis=1).reshape(batch, -1)
    back = jnp.pad(back, ((0, 0), (0, -back.shape[1] % HD))).reshape(batch, -1, HD)
    back = jnp.concatenate([dq_low, back], axis=1)
    back = jnp.broadcast_to(back, (half, *back.shape)).reshape(shards, -1, HD)
    spread = exchanged(back, VIS)
    dq_all = spread[:, :lines].reshape(heads, 2, text // heads // 2, width)
    row_stats = spread[:, lines:].reshape(shards, -1)[:, : 6 * lines].reshape(shards, 6, rows, GROUPS)
    row_stats = row_stats.transpose(1, 3, 0, 2).reshape(6, GROUPS, text)
    log_rows = whole_again([row_stats[k] for k in (0, 1, 2)])
    delta_rows = whole_again([row_stats[k] for k in (3, 4, 5)])

    part = jnp.einsum("hstq,zdq->hztsd", dq_all, weight, preferred_element_type=F32)
    part = part.astype(BF16).reshape(heads * 2, text // heads // 2, -1)
    arrived = exchanged(part, ("head", PAIR)).reshape(heads, batch, text // heads // 2, 2, -1)
    d_input = jnp.sum(arrived.astype(F32), axis=0).astype(BF16)
    d_input = d_input.transpose(0, 2, 1, 3).reshape(batch, text // heads, -1)

    d_keys, d_values = second_pass(
        low, centred, query, grad, jnp.exp(peak - log_rows), mean - delta_rows
    )
    d_kv = jnp.stack([d_keys, d_values])
    vis_rows = keys.shape[1]
    returned = swapped(d_kv[:, vis_rows:])
    d_kv = in_order(d_kv[:, :vis_rows], returned)
    return d_input, d_kv[:, 0], d_kv[:, 1]


def solution(mesh):
    torus = Mesh(
        mesh.devices.reshape(mesh.shape["head"], 8, 4, 2), ("head", "vis_0", "vis_1", "vis_2")
    )
    return jax.shard_map(
        per_device,
        mesh=torus,
        in_specs=(
            P(None, VIS, "head"),
            P(None, VIS, "head"),
            P(None, VIS, "head"),
            P(None, VIS, "head"),
            P(VIS, "head"),
        ),
        out_specs=(P(None, "head", VIS), P(None, VIS, "head"), P(None, VIS, "head")),
        check_vma=False,
    )
```

time: 490 us -> 181 us (0.37)
  waiting for transfers between devices: 269 us -> 44.7 us
  blocking collectives: 92.9 us -> 36.1 us
  starting transfers between devices: 69.2 us -> 43.7 us
  between operations: 14.2 us -> 1.13 us
  other arithmetic: 3.7 us -> 15.4 us
  local copies, waits for them, and re-layouts: 28.5 us -> 18.2 us
  matrix products: 11.5 us -> 20.8 us
    all_gather x1 -> x0, waiting for transfers between devices: 263 us -> none  [in_one_piece(): whole, at, outs = (lax.all_gather(both, axis, axis=dim, tiled=True), 0, [])]
    all_to_all x1 -> x3, waiting for transfers between devices: 6.58 us -> 44.7 us  [exchanged(): return lax.all_to_all(pieces, axes, split_axis=0, concat_axis=0, tiled=True)]
    all_to_all x1 -> x3, starting transfers between devices: 69.2 us -> 35.2 us  [exchanged(): return lax.all_to_all(pieces, axes, split_axis=0, concat_axis=0, tiled=True)]
    all_gather x3 -> x0, blocking collectives: 33.9 us -> none  [gathered_once(): both, at, found = (lax.all_gather(jnp.concatenate(lines), axis), 0, {})]
    all_to_all x2 -> x1, blocking collectives: 59 us -> 36.1 us  [exchanged(): return lax.all_to_all(pieces, axes, split_axis=0, concat_axis=0, tiled=True)]
    dot_general x29 -> x8, matrix products: 11.5 us -> 20.8 us  [the longest x1 5.65 us: first_pass(): jnp.einsum('jd,tgd->gjt', values, grad, preferred_element_type=F32)]
    convert_element_type x2 -> x3, other arithmetic: 1.41 us -> 10.6 us  [the longest x1 7.05 us: first_pass(): centred = (weights * (grad_probs - mean[:, None])).astype(BF16)]
    ppermute x0 -> x3, starting transfers between devices: none -> 8.51 us  [swapped(): return lax.ppermute(array, PAIR, [(0, 1), (1, 0)])]
  transfers between devices with their start and end apart: 2 -> 6, of which waited for: 2 -> 3; matrix products, arithmetic and copies ran while one was open for 0% -> 9% of each run, Pallas kernels for 0% -> 0%
where the time goes in v1:
time: 181 us; the launch traced here: 180 us
  waiting for transfers between devices  44.7 us (25%)
  starting transfers between devices  43.7 us (24%)
  blocking collectives  36.1 us (20%)
  matrix products  20.8 us (11%)
  local copies, waits for them, and re-layouts  18.2 us (10%)
  other arithmetic  15.4 us (9%)
    all_to_all x3, waiting for transfers between devices, exchanged(): return lax.all_to_all(pieces, axes, split_axis=0, concat_axis=0, tiled=True)  44.7 us
    all_to_all x1, blocking collectives, exchanged(): return lax.all_to_all(pieces, axes, split_axis=0, concat_axis=0, tiled=True)  36.1 us
    all_to_all x3, starting transfers between devices, exchanged(): return lax.all_to_all(pieces, axes, split_axis=0, concat_axis=0, tiled=True)  35.2 us
    ppermute x3, starting transfers between devices, swapped(): return lax.ppermute(array, PAIR, [(0, 1), (1, 0)])  8.51 us
    convert_element_type x1, other arithmetic, first_pass(): centred = (weights * (grad_probs - mean[:, None])).astype(BF16)  7.05 us
    dot_general x1, matrix products, first_pass(): jnp.einsum('jd,tgd->gjt', values, grad, preferred_element_type=F32)  5.65 us
    dot_general x1, matrix products, first_pass(): jnp.einsum('jd,tgd->gjt', keys, query, preferred_element_type=F32) * SCALE  3.76 us
  transfers between devices with their start and end apart: 6, of which 3 were waited for; matrix products, arithmetic and copies ran while one was open for 9% of the time, Pallas kernels for 0%

profile of v1, /device:TPU:1, one launch (start us, length us, event | category | flops | bytes accessed | tf_op | source)
XLA Modules:
  0.0 180.0 jit_solution(8546550565184903292)
XLA Ops:
  1.4 1.1 broadcast_in_dim.4
  2.5 12.9 %all-to-all-start = ((bf16[64,2,8,512]{3,2,1,0:T(8,128)(2,1)}), bf16[64,2,8,512]{3,2,1,0:T(8,128)(2,1)S(1)}, u32[]{:S(2)}, u32[]{:S(2)}) async-start(bf16[64,2,8,512]{3,2,1,0:T(8,128)(2,1)} %bitcast.12), calls=%async_computation | async-start | bytes 2097152 | tf_op jit(solution)/shard_map/all_to_all | solution.py:19
  15.5 2.9 %collective-permute-start.1 = (bf16[2,400,128]{2,1,0:T(8,128)(2,1)S(1)}, bf16[2,400,128]{2,1,0:T(8,128)(2,1)S(1)}, u32[]{:S(2)}, u32[]{:S(2)}) collective-permute-start(bf16[2,400,128]{2,1,0:T(8,128)(2,1)S(1)} %get-tuple-element.23), channel_id=1, source_target_pairs={{0,1},{1,0},{2,3},{3,2},{4,5},{5,4},{6,7},{7,6},{8,9},{9,8},{10,11... | collective-permute-start | bytes 614408 | tf_op jit(solution)/shard_map/ppermute | solution.py:23
  18.5 23.1 %all-to-all-done = bf16[64,2,8,512]{3,2,1,0:T(8,128)(2,1)S(1)} async-done(((bf16[64,2,8,512]{3,2,1,0:T(8,128)(2,1)}), bf16[64,2,8,512]{3,2,1,0:T(8,128)(2,1)S(1)}, u32[]{:S(2)}, u32[]{:S(2)}) %all-to-all-start) | async-done | bytes 1048608 | tf_op jit(solution)/shard_map/all_to_all | solution.py:19
  41.8 3.8 %bitcast_reduce_fusion = (f32[4,512]{1,0:T(4,128)S(1)}, f32[512,4,800]{0,2,1:T(8,128)}) fusion(bf16[2,400,128]{2,1,0:T(8,128)(2,1)S(1)} %get-tuple-element.24, bf16[2,400,128]{2,1,0:T(8,128)(2,1)S(1)} %collective-permute-done.1, bf16[512,4,128]{2,1,0:T(4,128)(2,1)S(1)} %reshape_squeeze.6), kind=kOutput, calls=%fused_computation.6 | convolution fusion | flops 423114752 | bytes 7495680 | tf_op jit(solution)/shard_map/jd,tgd->gjt/dot_general | solution.py:47
  45.7 5.7 %fusion = (f32[4,512]{1,0:T(4,128)S(1)}, f32[4,512]{1,0:T(4,128)S(1)}, f32[512,4,800]{0,2,1:T(8,128)}) fusion(f32[4,512]{1,0:T(4,128)S(1)} %get-tuple-element.32, f32[512,4,800]{0,2,1:T(8,128)} %get-tuple-element.35, bf16[2,400,128]{2,1,0:T(8,128)(2,1)S(1)} %collective-permute-done.1, bf16[2,400,128]{2,1,0:T(8,128)(2,1)S(1)} %get-tuple-element.24, ...), kind=kOutput, calls=%fused_computation.2 | convolution fusion | flops 428027904 | bytes 14065664 | tf_op jit(solution)/shard_map/jd,tgd->gjt/dot_general | solution.py:50
  52.9 7.1 %fusion.2 = (bf16[4,800,512]{2,1,0:T(8,128)(2,1)S(1)}, bf16[4,800,512]{2,1,0:T(8,128)(2,1)}) fusion(f32[512,4,800]{0,2,1:T(8,128)} %get-tuple-element.36, f32[4,512]{1,0:T(4,128)S(1)} %div.64, f32[4,512]{1,0:T(4,128)S(1)} %get-tuple-element.32, f32[512,4,800]{0,2,1:T(8,128)} %get-tuple-element.35), kind=kLoop, calls=%fused_computation.4 | loop fusion | flops 9830400 | bytes 19677184 | tf_op jit(solution)/shard_map/convert_element_type | solution.py:54
  60.0 1.5 fusion.6
  61.5 2.1 %copy.93 = bf16[512,4,128]{2,1,0:T(4,128)(2,1)} copy(bf16[512,4,128]{0,2,1:T(8,128)(2,1)} %fusion.6) | data formatting | bytes 1048576 | tf_op jit(solution)/shard_map/convert_element_type | solution.py:57
  63.6 3.6 %fusion.7 = bf16[512,4,128]{0,2,1:T(8,128)(2,1)} fusion(bf16[4,800,512]{2,1,0:T(8,128)(2,1)} %get-tuple-element.14, bf16[2,400,128]{2,1,0:T(8,128)(2,1)S(1)} %get-tuple-element.24, bf16[2,400,128]{2,1,0:T(8,128)(2,1)} %copy-done.4), kind=kOutput, calls=%fused_computation.15 | convolution fusion | flops 420102144 | bytes 4210688 | tf_op jit(solution)/shard_map/gjt,jd->tgd/dot_general | solution.py:56
  67.2 2.1 %copy.94 = bf16[512,4,128]{2,1,0:T(4,128)(2,1)} copy(bf16[512,4,128]{0,2,1:T(8,128)(2,1)} %fusion.7) | data formatting | bytes 1048576 | tf_op jit(solution)/shard_map/convert_element_type | solution.py:57
  71.7 1.3 pad_maximum_fusion
  73.0 36.1 %all_to_all.20 = bf16[64,66,128]{2,1,0:T(8,128)(2,1)S(1)} all-to-all(bf16[64,66,128]{2,1,0:T(8,128)(2,1)S(1)} %pad_maximum_fusion), channel_id=1, replica_groups=mesh['head'=8,'vis_0'=8,'vis_1'=4,'vis_2'=2] {'vis_0','vis_1','vis_2'}, dimensions={0} | all-to-all | bytes 2162688 | tf_op jit(solution)/shard_map/all_to_all | solution.py:19
  110.8 1.7 add_reduce_fusion
  113.6 8.5 %all-to-all-start.2 = ((bf16[64,34,128]{2,1,0:T(8,128)(2,1)}), bf16[64,34,128]{2,1,0:T(8,128)(2,1)}, u32[]{:S(2)}, u32[]{:S(2)}) async-start(bf16[64,34,128]{2,1,0:T(8,128)(2,1)} %bitcast.167), calls=%async_computation.2 | async-start | bytes 1310720 | tf_op jit(solution)/shard_map/all_to_all | solution.py:19
  122.1 3.0 %collective-permute-start = (bf16[64,512]{1,0:T(8,128)(2,1)}, bf16[64,512]{1,0:T(8,128)(2,1)}, u32[]{:S(2)}, u32[]{:S(2)}) collective-permute-start(bf16[64,512]{1,0:T(8,128)(2,1)} %param.9), channel_id=1, source_target_pairs={{0,1},{1,0},{2,3},{3,2},{4,5},{5,4},{6,7},{7,6},{8,9},{9,8},{10,11... | collective-permute-start | bytes 196616 | tf_op jit(solution)/shard_map/ppermute | solution.py:23
  125.1 14.1 %all-to-all-done.2 = bf16[64,34,128]{2,1,0:T(8,128)(2,1)} async-done(((bf16[64,34,128]{2,1,0:T(8,128)(2,1)}), bf16[64,34,128]{2,1,0:T(8,128)(2,1)}, u32[]{:S(2)}, u32[]{:S(2)}) %all-to-all-start.2) | async-done | bytes 557088 | tf_op jit(solution)/shard_map/all_to_all | solution.py:19
  141.8 3.6 %fusion.15 = (bf16[512,4,128]{2,1,0:T(4,128)(2,1)S(1)}, bf16[512,4,128]{2,1,0:T(4,128)(2,1)S(1)}, bf16[512,4,128]{2,1,0:T(4,128)(2,1)S(1)}) fusion(bf16[512,4,128]{2,1,0:T(4,128)(2,1)} %copy-done.1, f32[512,4]{1,0:T(8,128)S(1)} %copy.113, f32[512,4]{1,0:T(8,128)} %copy.116, bf16[512,4,128]{2,1,0:T(4,128)(2,1)} %copy-done.2), kind=kLoop, calls=%fused_computation.28 | loop fusion | flops 2097152 | bytes 2637824 | tf_op jit(solution)/shard_map/convert_element_type | solution.py:63
  145.4 3.1 %fusion.14 = bf16[1,800,128]{2,1,0:T(8,128)(2,1)S(1)} fusion(bf16[4,800,512]{2,1,0:T(8,128)(2,1)} %get-tuple-element.14, bf16[512,4,128]{2,1,0:T(4,128)(2,1)S(1)} %get-tuple-element.25), kind=kOutput, calls=%fused_computation.27 | convolution fusion | flops 419532800 | bytes 4005888 | tf_op jit(solution)/shard_map/gjt,tgd->jd/dot_general | solution.py:65
  150.6 2.5 %collective-permute-start.2 = (bf16[2,400,128]{2,1,0:T(8,128)(2,1)S(1)}, bf16[2,400,128]{2,1,0:T(8,128)(2,1)S(1)}, u32[]{:S(2)}, u32[]{:S(2)}) collective-permute-start(bf16[2,400,128]{2,1,0:T(8,128)(2,1)S(1)} %get-tuple-element.22), channel_id=1, source_target_pairs={{0,1},{1,0},{2,3},{3,2},{4,5},{5,4},{6,7},{7,6},{8,9},{9,8},{10,11... | collective-permute-start | bytes 614408 | tf_op jit(solution)/shard_map/ppermute | solution.py:23
  153.2 1.1 slice.140
  154.6 1.2 fusion.12
  156.9 13.8 %all-to-all-start.3 = ((bf16[16,32,128]{2,1,0:T(8,128)(2,1)}), bf16[16,32,128]{2,1,0:T(8,128)(2,1)S(1)}, u32[]{:S(2)}, u32[]{:S(2)}) async-start(bf16[16,32,128]{2,1,0:T(8,128)(2,1)} %reshape.376), calls=%async_computation.3 | async-start | bytes 262144 | tf_op jit(solution)/shard_map/all_to_all | solution.py:19
  171.5 7.4 %all-to-all-done.3 = bf16[16,32,128]{2,1,0:T(8,128)(2,1)S(1)} async-done(((bf16[16,32,128]{2,1,0:T(8,128)(2,1)}), bf16[16,32,128]{2,1,0:T(8,128)(2,1)S(1)}, u32[]{:S(2)}, u32[]{:S(2)}) %all-to-all-start.3) | async-done | bytes 131104 | tf_op jit(solution)/shard_map/all_to_all | solution.py:19
  (90 shorter events, 15.6 us)
Async XLA Ops:
  0.6 14.8 %copy-start.7 = (bf16[2,400,128]{2,1,0:T(8,128)(2,1)S(1)}, bf16[2,400,128]{2,1,0:T(8,128)(2,1)}, u32[]{:S(2)}) copy-start(bf16[2,400,128]{2,1,0:T(8,128)(2,1)} %param.6) | copy-start | bytes 614404
  0.6 14.8 %copy-start.6 = (bf16[2,400,128]{2,1,0:T(8,128)(2,1)S(1)}, bf16[2,400,128]{2,1,0:T(8,128)(2,1)}, u32[]{:S(2)}) copy-start(bf16[2,400,128]{2,1,0:T(8,128)(2,1)} %param.7) | copy-start | bytes 614404
  2.5 39.0 %all-to-all-start = ((bf16[64,2,8,512]{3,2,1,0:T(8,128)(2,1)}), bf16[64,2,8,512]{3,2,1,0:T(8,128)(2,1)S(1)}, u32[]{:S(2)}, u32[]{:S(2)}) async-start(bf16[64,2,8,512]{3,2,1,0:T(8,128)(2,1)} %bitcast.12), calls=%async_computation | async-start | bytes 2097152 | tf_op jit(solution)/shard_map/all_to_all | solution.py:19
  15.5 26.3 %collective-permute-start.1 = (bf16[2,400,128]{2,1,0:T(8,128)(2,1)S(1)}, bf16[2,400,128]{2,1,0:T(8,128)(2,1)S(1)}, u32[]{:S(2)}, u32[]{:S(2)}) collective-permute-start(bf16[2,400,128]{2,1,0:T(8,128)(2,1)S(1)} %get-tuple-element.23), channel_id=1, source_target_pairs={{0,1},{1,0},{2,3},{3,2},{4,5},{5,4},{6,7},{7,6},{8,9},{9,8},{10,11... | collective-permute-start | bytes 614408 | tf_op jit(solution)/shard_map/ppermute | solution.py:23
  41.8 3.8 %copy-start.1 = (bf16[512,4,128]{2,1,0:T(4,128)(2,1)}, bf16[512,4,128]{2,1,0:T(4,128)(2,1)S(1)}, u32[]{:S(2)}) copy-start(bf16[512,4,128]{2,1,0:T(4,128)(2,1)S(1)} %reshape_squeeze.6) | copy-start | bytes 1572868
  41.8 3.9 %copy-start.4 = (bf16[2,400,128]{2,1,0:T(8,128)(2,1)}, bf16[2,400,128]{2,1,0:T(8,128)(2,1)S(1)}, u32[]{:S(2)}) copy-start(bf16[2,400,128]{2,1,0:T(8,128)(2,1)S(1)} %collective-permute-done.1) | copy-start | bytes 614404
  45.7 5.7 %copy-start.2 = (bf16[512,4,128]{2,1,0:T(4,128)(2,1)}, bf16[512,4,128]{2,1,0:T(4,128)(2,1)S(1)}, u32[]{:S(2)}) copy-start(bf16[512,4,128]{2,1,0:T(4,128)(2,1)S(1)} %reshape_squeeze.7) | copy-start | bytes 1572868
  52.9 7.1 %copy-start.5 = (bf16[2,400,128]{2,1,0:T(8,128)(2,1)S(1)}, bf16[2,400,128]{2,1,0:T(8,128)(2,1)}, u32[]{:S(2)}) copy-start(bf16[2,400,128]{2,1,0:T(8,128)(2,1)} %copy-done.4) | copy-start | bytes 614404
  109.1 1.0 copy-start.3
  113.6 25.6 %all-to-all-start.2 = ((bf16[64,34,128]{2,1,0:T(8,128)(2,1)}), bf16[64,34,128]{2,1,0:T(8,128)(2,1)}, u32[]{:S(2)}, u32[]{:S(2)}) async-start(bf16[64,34,128]{2,1,0:T(8,128)(2,1)} %bitcast.167), calls=%async_computation.2 | async-start | bytes 1310720 | tf_op jit(solution)/shard_map/all_to_all | solution.py:19
  122.1 32.5 %collective-permute-start = (bf16[64,512]{1,0:T(8,128)(2,1)}, bf16[64,512]{1,0:T(8,128)(2,1)}, u32[]{:S(2)}, u32[]{:S(2)}) collective-permute-start(bf16[64,512]{1,0:T(8,128)(2,1)} %param.9), channel_id=1, source_target_pairs={{0,1},{1,0},{2,3},{3,2},{4,5},{5,4},{6,7},{7,6},{8,9},{9,8},{10,11... | collective-permute-start | bytes 196616 | tf_op jit(solution)/shard_map/ppermute | solution.py:23
  145.4 3.1 %copy-start = (bf16[4,800,512]{2,1,0:T(8,128)(2,1)S(1)}, bf16[4,800,512]{2,1,0:T(8,128)(2,1)}, u32[]{:S(2)}) copy-start(bf16[4,800,512]{2,1,0:T(8,128)(2,1)} %get-tuple-element.14) | copy-start | bytes 9830404
  149.5 5.1 %copy-start.8 = (bf16[64,512]{1,0:T(8,128)(2,1)S(1)}, bf16[64,512]{1,0:T(8,128)(2,1)}, u32[]{:S(2)}) copy-start(bf16[64,512]{1,0:T(8,128)(2,1)} %param.9) | copy-start | bytes 196612
  150.6 20.1 %collective-permute-start.2 = (bf16[2,400,128]{2,1,0:T(8,128)(2,1)S(1)}, bf16[2,400,128]{2,1,0:T(8,128)(2,1)S(1)}, u32[]{:S(2)}, u32[]{:S(2)}) collective-permute-start(bf16[2,400,128]{2,1,0:T(8,128)(2,1)S(1)} %get-tuple-element.22), channel_id=1, source_target_pairs={{0,1},{1,0},{2,3},{3,2},{4,5},{5,4},{6,7},{7,6},{8,9},{9,8},{10,11... | collective-permute-start | bytes 614408 | tf_op jit(solution)/shard_map/ppermute | solution.py:23
  156.9 22.1 %all-to-all-start.3 = ((bf16[16,32,128]{2,1,0:T(8,128)(2,1)}), bf16[16,32,128]{2,1,0:T(8,128)(2,1)S(1)}, u32[]{:S(2)}, u32[]{:S(2)}) async-start(bf16[16,32,128]{2,1,0:T(8,128)(2,1)} %reshape.376), calls=%async_computation.3 | async-start | bytes 262144 | tf_op jit(solution)/shard_map/all_to_all | solution.py:19

commit v2 on v1

v2 whole, which is shorter than its diff:
```python
import jax
import jax.numpy as jnp
from jax import lax
from jax.sharding import Mesh
from jax.sharding import PartitionSpec as P

HQ = 32
KVH = 8
HD = 128
GROUPS = HQ // KVH
ALONG = "vis_0"
GROUP = ("vis_1", "vis_2")
VIS = (ALONG, *GROUP)
SCALE = HD ** (-0.5)
BF16 = jnp.bfloat16
F32 = jnp.float32


def exchanged(pieces, axes):
    return lax.all_to_all(pieces, axes, split_axis=0, concat_axis=0, tiled=True)


def copies(array, count):
    return jnp.broadcast_to(array, (count, *array.shape))


def rounded(array):
    return lax.reduce_precision(array, exponent_bits=8, mantissa_bits=7)


def in_pieces(array, count):
    out = []
    for _ in range(count):
        piece = rounded(array)
        out.append(piece.astype(BF16))
        array = array - piece
    return out


def whole_again(pieces):
    total = pieces[-1].astype(F32)
    for piece in reversed(pieces[:-1]):
        total = total + piece.astype(F32)
    return total


def first_pass(query, grad, keys, values):
    scores = jnp.einsum("jd,td->jt", keys, query, preferred_element_type=F32) * SCALE
    peak = rounded(jnp.max(scores, axis=0))
    weights = jnp.exp(scores - peak)
    grad_probs = jnp.einsum("jd,td->jt", values, grad, preferred_element_type=F32)
    total = jnp.sum(weights, axis=0)
    mean = jnp.sum(weights * grad_probs, axis=0) / total
    low = weights.astype(BF16)
    centred = (weights * (grad_probs - mean)).astype(BF16)
    term_a = jnp.einsum("jt,jd->td", centred, keys, preferred_element_type=F32)
    term_b = jnp.einsum("jt,jd->td", low, keys, preferred_element_type=F32)
    terms = jnp.concatenate([term_a.astype(BF16), term_b.astype(BF16)], axis=1)
    return peak, total, mean, low, centred, terms


def second_pass(low, centred, query, grad, scale, shift):
    by_row = scale[:, None]
    grad_scaled = (grad.astype(F32) * by_row).astype(BF16)
    query_scaled = (query.astype(F32) * (by_row * SCALE)).astype(BF16)
    query_shifted = (query.astype(F32) * ((scale * shift)[:, None] * SCALE)).astype(BF16)
    d_values = jnp.einsum("jt,td->jd", low, grad_scaled, preferred_element_type=F32)
    d_keys = jnp.einsum("jt,td->jd", centred, query_scaled, preferred_element_type=F32)
    d_keys = d_keys + jnp.einsum("jt,td->jd", low, query_shifted, preferred_element_type=F32)
    return jnp.concatenate([d_keys.astype(BF16), d_values.astype(BF16)], axis=1)


def per_device(queries, keys, values, d_out, q_weight):
    batch, rows, width = queries.shape
    vis_rows = keys.shape[1]
    d_rows = q_weight.shape[0]
    heads = lax.axis_size("head")
    steps = lax.axis_size(ALONG)
    group = lax.axis_size(GROUP)
    text = rows * steps * group
    block = text // steps
    here = lax.axis_index(ALONG)

    def by_head(array):
        return array.reshape(batch, rows, GROUPS, HD).transpose(2, 0, 1, 3)

    sent = jnp.concatenate([by_head(queries), by_head(d_out)], axis=-1).reshape(group, rows, 2 * HD)
    sent = copies(sent, steps).reshape(steps * group, rows, 2 * HD)
    whole = exchanged(sent, VIS).reshape(text, 2 * HD)

    key_values = copies(jnp.concatenate([keys, values], axis=-1), GROUPS)
    key_values = key_values.reshape(group, vis_rows, 2 * HD)
    weight = q_weight.reshape(2, d_rows // 2, GROUPS, HD).transpose(2, 1, 0, 3)
    weight = jnp.repeat(weight.reshape(GROUPS, d_rows // 2, 2 * HD), batch, axis=0)
    near = exchanged(jnp.concatenate([key_values, weight], axis=1), GROUP)
    kv = near[:, :vis_rows].reshape(group * vis_rows, 2 * HD)
    weight = near[:, vis_rows:].reshape(group, d_rows // 2, 2, HD).transpose(0, 2, 1, 3)
    weight = weight.reshape(group, d_rows, HD)
    blank = jnp.zeros_like(weight)
    weight = jnp.concatenate(
        [jnp.concatenate([weight, blank], axis=2), jnp.concatenate([blank, weight], axis=2)], axis=1
    )

    query, grad = whole[:, :HD], whole[:, HD:]
    peak, total, mean, low, centred, terms = first_pass(query, grad, kv[:, :HD], kv[:, HD:])

    stats = jnp.stack(in_pieces(peak, 1) + in_pieces(total, 2) + in_pieces(mean, 3))
    stats = stats.reshape(-1, 2 * HD)
    parcel = [terms.reshape(steps, block, 2 * HD), copies(stats, steps)]
    home = exchanged(jnp.concatenate(parcel, axis=1), ALONG)
    home_terms = home[:, :block].astype(F32)
    home_stats = home[:, block:].reshape(steps, 6, text)
    peaks = home_stats[:, 0].astype(F32)
    totals = whole_again([home_stats[:, k] for k in (1, 2)])
    means = whole_again([home_stats[:, k] for k in (3, 4, 5)])
    peak_all = jnp.max(peaks, axis=0)
    factor = jnp.exp(peaks - peak_all)
    share = factor * totals
    total_all = jnp.sum(share, axis=0)
    delta = jnp.sum(share * means, axis=0) / total_all
    factor = factor / total_all
    shift = means - delta

    mine = lax.dynamic_slice_in_dim(jnp.stack([factor, factor * shift]), here * block, block, 2)
    dq = jnp.sum(
        mine[0][..., None] * home_terms[..., :HD] + mine[1][..., None] * home_terms[..., HD:], axis=0
    )
    dq_low = (dq * SCALE).astype(BF16).reshape(2, block // 2, HD).transpose(1, 0, 2)
    dq_low = dq_low.reshape(block // 2, 2 * HD)
    dq_all = exchanged(copies(dq_low, steps), ALONG)

    part = jnp.einsum("hrk,snk->hsrn", dq_all, weight, preferred_element_type=F32).astype(BF16)
    part = part.reshape(heads * group, block // 2, 2 * d_rows)
    arrived = exchanged(part, ("head", *GROUP))
    arrived = arrived.reshape(heads * GROUPS, batch, block // 2, 2, d_rows)
    d_input = jnp.sum(arrived.astype(F32), axis=0).astype(BF16)
    d_input = d_input.transpose(0, 2, 1, 3).reshape(batch, block, d_rows)

    scale = lax.dynamic_index_in_dim(factor, here, 0, keepdims=False)
    moved = lax.dynamic_index_in_dim(shift, here, 0, keepdims=False)
    d_kv = second_pass(low, centred, query, grad, scale, moved).reshape(group, vis_rows, 2 * HD)
    d_kv = exchanged(d_kv, GROUP).reshape(GROUPS, batch, vis_rows, 2 * HD)
    d_kv = jnp.sum(d_kv.astype(F32), axis=0).astype(BF16)
    return d_input, d_kv[..., :HD], d_kv[..., HD:]


def solution(mesh):
    torus = Mesh(
        mesh.devices.reshape(mesh.shape["head"], 8, 4, 2), ("head", "vis_0", "vis_1", "vis_2")
    )
    return jax.shard_map(
        per_device,
        mesh=torus,
        in_specs=(
            P(None, VIS, "head"),
            P(None, VIS, "head"),
            P(None, VIS, "head"),
            P(None, VIS, "head"),
            P(VIS, "head"),
        ),
        out_specs=(P(None, "head", VIS), P(None, VIS, "head"), P(None, VIS, "head")),
        check_vma=False,
    )
```

time: 181 us -> 168 us (0.928)
  blocking collectives: 36.1 us -> 0 us
  waiting for transfers between devices: 44.7 us -> 71.4 us
  local copies, waits for them, and re-layouts: 18.2 us -> 12.7 us
  starting transfers between devices: 43.7 us -> 48.4 us
  matrix products: 20.8 us -> 17.5 us
    all_to_all x1 -> x0, blocking collectives: 36.1 us -> none  [exchanged(): return lax.all_to_all(pieces, axes, split_axis=0, concat_axis=0, tiled=True)]
    all_to_all x3 -> x6, waiting for transfers between devices: 44.7 us -> 71.4 us  [exchanged(): return lax.all_to_all(pieces, axes, split_axis=0, concat_axis=0, tiled=True)]
    all_to_all x3 -> x6, starting transfers between devices: 35.2 us -> 48.4 us  [exchanged(): return lax.all_to_all(pieces, axes, split_axis=0, concat_axis=0, tiled=True)]
    ppermute x3 -> x0, starting transfers between devices: 8.51 us -> none  [swapped(): return lax.ppermute(array, PAIR, [(0, 1), (1, 0)])]
    concatenate x0 -> x3, local copies, waits for them, and re-layouts: none -> 4.06 us  [the longest x1 2.26 us: second_pass(): return jnp.concatenate([d_keys.astype(BF16), d_values.astype(BF16)], axis=1)]
    concatenate x2 -> x6, other arithmetic: 1.31 us -> 4.98 us  [the longest x1 1.7 us: per_device(): home = exchanged(jnp.concatenate(parcel, axis=1), ALONG)]
    convert_element_type x3 -> x1, local copies, waits for them, and re-layouts: 4.44 us -> 0.84 us  [per_device(): jnp.einsum('hrk,snk->hsrn', dq_all, weight, preferred_element_type=F32)]
    reduce_sum x4 -> x0, local copies, waits for them, and re-layouts: 3.47 us -> none  [the longest x2 1.74 us: first_pass(): total = jnp.sum(weights, axis=1)]
  transfers between devices with their start and end apart: 6 -> 6, of which waited for: 3 -> 6; matrix products, arithmetic and copies ran while one was open for 9% -> 10% of each run, Pallas kernels for 0% -> 0%
where the time goes in v2:
time: 168 us; the launch traced here: 167 us
  waiting for transfers between devices  71.4 us (43%)
  starting transfers between devices  48.4 us (29%)
  matrix products  17.5 us (10%)
  other arithmetic  16.2 us (10%)
  local copies, waits for them, and re-layouts  12.7 us (8%)
    all_to_all x6, waiting for transfers between devices, exchanged(): return lax.all_to_all(pieces, axes, split_axis=0, concat_axis=0, tiled=True)  71.4 us
    all_to_all x6, starting transfers between devices, exchanged(): return lax.all_to_all(pieces, axes, split_axis=0, concat_axis=0, tiled=True)  48.4 us
    convert_element_type x1, other arithmetic, first_pass(): centred = (weights * (grad_probs - mean)).astype(BF16)  6.74 us
    dot_general x1, matrix products, first_pass(): jnp.einsum('jd,td->jt', values, grad, preferred_element_type=F32)  5.37 us
    dot_general x1, matrix products, second_pass(): jnp.einsum('jt,td->jd', centred, query_scaled, preferred_element_type=F32)  4.29 us
  transfers between devices with their start and end apart: 6, of which 6 were waited for; matrix products, arithmetic and copies ran while one was open for 10% of the time, Pallas kernels for 0%

profile of v2, /device:TPU:1, one launch (start us, length us, event | category | flops | bytes accessed | tf_op | source)
XLA Modules:
  0.0 167.3 jit_solution(5849470414294544649)
XLA Ops:
  2.9 1.4 pad_maximum_fusion
  4.2 6.6 %all-to-all-start = ((bf16[8,432,256]{2,1,0:T(8,128)(2,1)}), bf16[8,432,256]{2,1,0:T(8,128)(2,1)S(1)}, u32[]{:S(2)}, u32[]{:S(2)}) async-start(bf16[8,432,256]{2,1,0:T(8,128)(2,1)} %pad_maximum_fusion), calls=%async_computation | async-start | bytes 3538944 | tf_op jit(solution)/shard_map/all_to_all | solution.py:20
  10.9 19.8 %all-to-all-done = bf16[8,432,256]{2,1,0:T(8,128)(2,1)S(1)} async-done(((bf16[8,432,256]{2,1,0:T(8,128)(2,1)}), bf16[8,432,256]{2,1,0:T(8,128)(2,1)S(1)}, u32[]{:S(2)}, u32[]{:S(2)}) %all-to-all-start) | async-done | bytes 1769504 | tf_op jit(solution)/shard_map/all_to_all | solution.py:20
  31.5 13.0 %all-to-all-start.1 = ((bf16[64,8,256]{2,1,0:T(8,128)(2,1)}), bf16[64,8,256]{2,1,0:T(8,128)(2,1)}, u32[]{:S(2)}, u32[]{:S(2)}) async-start(bf16[64,8,256]{2,1,0:T(8,128)(2,1)} %bitcast.13), calls=%async_computation.1 | async-start | bytes 524288 | tf_op jit(solution)/shard_map/all_to_all | solution.py:20
  44.6 10.4 %all-to-all-done.1 = bf16[64,8,256]{2,1,0:T(8,128)(2,1)} async-done(((bf16[64,8,256]{2,1,0:T(8,128)(2,1)}), bf16[64,8,256]{2,1,0:T(8,128)(2,1)}, u32[]{:S(2)}, u32[]{:S(2)}) %all-to-all-start.1) | async-done | bytes 262176 | tf_op jit(solution)/shard_map/all_to_all | solution.py:20
  55.1 1.9 %fusion.54 = (f32[512]{0:T(512)S(1)}, f32[3200,512]{1,0:T(8,128)S(1)}) fusion(bf16[512,256]{1,0:T(8,128)(2,1)} %bitcast.14, bf16[3200,256]{1,0:T(8,128)(2,1)S(1)} %bitcast.87), kind=kOutput, calls=%fused_computation.97 | convolution fusion | flops 422706688 | bytes 7505920 | tf_op jit(solution)/shard_map/jd,td->jt/dot_general | solution.py:48
  57.1 5.4 %multiply_reduce_fusion = (f32[512]{0:T(512)S(1)}, f32[512]{0:T(512)S(1)}, f32[3200,512]{1,0:T(8,128)}) fusion(f32[3200,512]{1,0:T(8,128)S(1)} %get-tuple-element.28, f32[512]{0:T(512)S(1)} %get-tuple-element.25, bf16[512,256]{1,0:T(8,128)(2,1)} %bitcast.14, bf16[3200,256]{1,0:T(8,128)(2,1)S(1)} %bitcast.88), kind=kOutput, calls=%fused_computation.2 | convolution fusion | flops 425982976 | bytes 14063616 | tf_op jit(solution)/shard_map/jd,td->jt/dot_general | solution.py:51
  62.5 6.7 %multiply_convert_fusion = (bf16[3200,512]{1,0:T(8,128)(2,1)S(1)}, bf16[3200,512]{1,0:T(8,128)(2,1)S(1)}) fusion(f32[3200,512]{1,0:T(8,128)} %get-tuple-element.29, f32[3200,512]{1,0:T(8,128)} %copy-done, f32[512]{0:T(512)S(1)} %div.53, f32[512]{0:T(512)S(1)} %get-tuple-element.25), kind=kLoop, calls=%fused_computation.1 | loop fusion | flops 8192000 | bytes 19664896 | tf_op jit(solution)/shard_map/convert_element_type | solution.py:55
  71.7 1.8 %copy.33 = bf16[512,256]{1,0:T(8,128)(2,1)} copy(bf16[512,256]{0,1:T(8,128)(2,1)} %pad_maximum_fusion.4) | data formatting | bytes 524288 | tf_op jit(solution)/shard_map/concatenate | solution.py:58
  73.5 1.7 %pad_maximum_fusion.3 = bf16[8,76,256]{2,1,0:T(8,128)(2,1)} fusion(bf16[8,12,256]{2,1,0:T(8,128)(2,1)S(1)} %broadcast_in_dim.28, bf16[8,64,256]{2,1,0:T(8,128)(2,1)} %bitcast.94), kind=kLoop, calls=%fused_computation.32 | loop fusion | flops 622592 | bytes 622592 | tf_op jit(solution)/shard_map/concatenate | solution.py:110
  75.2 4.9 %all-to-all-start.2 = ((bf16[8,76,256]{2,1,0:T(8,128)(2,1)}), bf16[8,76,256]{2,1,0:T(8,128)(2,1)}, u32[]{:S(2)}, u32[]{:S(2)}) async-start(bf16[8,76,256]{2,1,0:T(8,128)(2,1)} %pad_maximum_fusion.3), calls=%async_computation.2 | async-start | bytes 655360 | tf_op jit(solution)/shard_map/all_to_all | solution.py:20
  80.2 10.4 %all-to-all-done.2 = bf16[8,76,256]{2,1,0:T(8,128)(2,1)} async-done(((bf16[8,76,256]{2,1,0:T(8,128)(2,1)}), bf16[8,76,256]{2,1,0:T(8,128)(2,1)}, u32[]{:S(2)}, u32[]{:S(2)}) %all-to-all-start.2) | async-done | bytes 311328 | tf_op jit(solution)/shard_map/all_to_all | solution.py:20
  94.1 3.4 %all-to-all-start.3 = ((bf16[8,32,256]{2,1,0:T(8,128)(2,1)}), bf16[8,32,256]{2,1,0:T(8,128)(2,1)S(1)}, u32[]{:S(2)}, u32[]{:S(2)}) async-start(bf16[8,32,256]{2,1,0:T(8,128)(2,1)} %broadcast_in_dim.29), calls=%async_computation.3 | async-start | bytes 262144 | tf_op jit(solution)/shard_map/all_to_all | solution.py:20
  98.3 4.3 %fusion.24 = f32[3200,128]{0,1:T(8,128)} fusion(bf16[3200,512]{1,0:T(8,128)(2,1)} %copy-done.1, f32[512]{0:T(512)S(1)} %get-tuple-element.20, bf16[512,256]{1,0:T(8,128)(2,1)} %bitcast.14), kind=kOutput, calls=%fused_computation.43 | convolution fusion | flops 419627008 | bytes 5048320 | tf_op jit(solution)/shard_map/jt,td->jd/dot_general | solution.py:68
  102.5 2.8 %all-to-all-done.3 = bf16[8,32,256]{2,1,0:T(8,128)(2,1)S(1)} async-done(((bf16[8,32,256]{2,1,0:T(8,128)(2,1)}), bf16[8,32,256]{2,1,0:T(8,128)(2,1)S(1)}, u32[]{:S(2)}, u32[]{:S(2)}) %all-to-all-start.3) | async-done | bytes 131104 | tf_op jit(solution)/shard_map/all_to_all | solution.py:20
  106.5 16.1 %all-to-all-start.4 = ((bf16[64,32,128]{2,1,0:T(8,128)(2,1)}), bf16[64,32,128]{2,1,0:T(8,128)(2,1)}, u32[]{:S(2)}, u32[]{:S(2)}) async-start(bf16[64,32,128]{2,1,0:T(8,128)(2,1)} %bitcast.93), calls=%async_computation.4 | async-start | bytes 1048576 | tf_op jit(solution)/shard_map/all_to_all | solution.py:20
  122.6 2.2 %convolution_convert_fusion = bf16[3200,128]{0,1:T(8,128)(2,1)S(1)} fusion(bf16[3200,512]{1,0:T(8,128)(2,1)S(1)} %get-tuple-element.11, f32[512]{0:T(512)S(1)} %bitcast.108, bf16[512,256]{1,0:T(8,128)(2,1)} %bitcast.14), kind=kOutput, calls=%fused_computation.6 | convolution fusion | flops 420036608 | bytes 4229120 | tf_op jit(solution)/shard_map/jt,td->jd/dot_general | solution.py:67
  124.8 2.1 %fusion = bf16[3200,128]{0,1:T(8,128)(2,1)S(1)} fusion(f32[3200,128]{0,1:T(8,128)S(1)} %copy-done.5, bf16[3200,512]{1,0:T(8,128)(2,1)S(1)} %get-tuple-element.11, f32[512]{0:T(512)S(1)} %get-tuple-element.19, bf16[512,256]{1,0:T(8,128)(2,1)} %bitcast.14), kind=kOutput, calls=%fused_computation.5 | convolution fusion | flops 420446208 | bytes 5867520 | tf_op jit(solution)/shard_map/jt,td->jd/dot_general | solution.py:69
  127.0 2.3 %copy.38 = bf16[3200,256]{1,0:T(8,128)(2,1)} copy(bf16[3200,256]{0,1:T(8,128)(2,1)S(1)} %pad_maximum_fusion.1) | data formatting | bytes 3276800 | tf_op jit(solution)/shard_map/concatenate | solution.py:70
  129.3 10.6 %all-to-all-done.4 = bf16[64,32,128]{2,1,0:T(8,128)(2,1)} async-done(((bf16[64,32,128]{2,1,0:T(8,128)(2,1)}), bf16[64,32,128]{2,1,0:T(8,128)(2,1)}, u32[]{:S(2)}, u32[]{:S(2)}) %all-to-all-start.4) | async-done | bytes 524320 | tf_op jit(solution)/shard_map/all_to_all | solution.py:20
  139.9 4.4 %all-to-all-start.5 = ((bf16[8,400,256]{2,1,0:T(8,128)(2,1)}), bf16[8,400,256]{2,1,0:T(8,128)(2,1)S(1)}, u32[]{:S(2)}, u32[]{:S(2)}) async-start(bf16[8,400,256]{2,1,0:T(8,128)(2,1)} %bitcast.35), calls=%async_computation.5 | async-start | bytes 3276800 | tf_op jit(solution)/shard_map/all_to_all | solution.py:20
  144.4 2.4 %reshape.404 = bf16[32,2,32,2,64]{4,3,2,1,0:T(2,128)(2,1)S(1)} reshape(bf16[64,32,128]{2,1,0:T(8,128)(2,1)} %all-to-all-done.4) | data formatting | bytes 1048576 | tf_op jit(solution)/shard_map/reshape | solution.py:135
  146.8 1.3 reduce_sum.80
  148.7 17.3 %all-to-all-done.5 = bf16[8,400,256]{2,1,0:T(8,128)(2,1)S(1)} async-done(((bf16[8,400,256]{2,1,0:T(8,128)(2,1)}), bf16[8,400,256]{2,1,0:T(8,128)(2,1)S(1)}, u32[]{:S(2)}, u32[]{:S(2)}) %all-to-all-start.5) | async-done | bytes 1638432 | tf_op jit(solution)/shard_map/all_to_all | solution.py:20
  (63 shorter events, 13.0 us)
Async XLA Ops:
  2.8 8.0 %copy-start.6 = (bf16[2,8,512]{2,1,0:T(8,128)(2,1)S(1)}, bf16[2,8,512]{2,1,0:T(8,128)(2,1)}, u32[]{:S(2)}) copy-start(bf16[2,8,512]{2,1,0:T(8,128)(2,1)} %param.8) | copy-start | bytes 49156
  2.8 8.0 %copy-start.7 = (bf16[2,8,512]{2,1,0:T(8,128)(2,1)S(1)}, bf16[2,8,512]{2,1,0:T(8,128)(2,1)}, u32[]{:S(2)}) copy-start(bf16[2,8,512]{2,1,0:T(8,128)(2,1)} %param.5) | copy-start | bytes 49156
  4.2 26.5 %all-to-all-start = ((bf16[8,432,256]{2,1,0:T(8,128)(2,1)}), bf16[8,432,256]{2,1,0:T(8,128)(2,1)S(1)}, u32[]{:S(2)}, u32[]{:S(2)}) async-start(bf16[8,432,256]{2,1,0:T(8,128)(2,1)} %pad_maximum_fusion), calls=%async_computation | async-start | bytes 3538944 | tf_op jit(solution)/shard_map/all_to_all | solution.py:20
  30.7 26.3 %copy-start.4 = (bf16[8,432,256]{2,1,0:T(8,128)(2,1)}, bf16[8,432,256]{2,1,0:T(8,128)(2,1)S(1)}, u32[]{:S(2)}) copy-start(bf16[8,432,256]{2,1,0:T(8,128)(2,1)S(1)} %all-to-all-done) | copy-start | bytes 5308420
  31.5 23.6 %all-to-all-start.1 = ((bf16[64,8,256]{2,1,0:T(8,128)(2,1)}), bf16[64,8,256]{2,1,0:T(8,128)(2,1)}, u32[]{:S(2)}, u32[]{:S(2)}) async-start(bf16[64,8,256]{2,1,0:T(8,128)(2,1)} %bitcast.13), calls=%async_computation.1 | async-start | bytes 524288 | tf_op jit(solution)/shard_map/all_to_all | solution.py:20
  44.6 12.4 %copy-start.2 = (bf16[8,400,256]{2,1,0:T(8,128)(2,1)}, bf16[8,400,256]{2,1,0:T(8,128)(2,1)S(1)}, u32[]{:S(2)}) copy-start(bf16[8,400,256]{2,1,0:T(8,128)(2,1)S(1)} %slice.81) | copy-start | bytes 4915204
  57.0 5.4 %copy-start = (f32[3200,512]{1,0:T(8,128)}, f32[3200,512]{1,0:T(8,128)S(1)}, u32[]{:S(2)}) copy-start(f32[3200,512]{1,0:T(8,128)S(1)} %get-tuple-element.28) | copy-start | bytes 19660804
  62.5 6.8 %copy-start.3 = (bf16[8,400,256]{2,1,0:T(8,128)(2,1)S(1)}, bf16[8,400,256]{2,1,0:T(8,128)(2,1)}, u32[]{:S(2)}) copy-start(bf16[8,400,256]{2,1,0:T(8,128)(2,1)} %copy-done.2) | copy-start | bytes 4915204
  69.3 1.7 %copy-start.1 = (bf16[3200,512]{1,0:T(8,128)(2,1)}, bf16[3200,512]{1,0:T(8,128)(2,1)S(1)}, u32[]{:S(2)}) copy-start(bf16[3200,512]{1,0:T(8,128)(2,1)S(1)} %get-tuple-element.10) | copy-start | bytes 9830404
  70.0 10.1 %slice-start = ((bf16[8,432,256]{2,1,0:T(8,128)(2,1)}), bf16[8,32,256]{2,1,0:T(8,128)(2,1)S(1)}, s32[]{:S(2)}) async-start(bf16[8,432,256]{2,1,0:T(8,128)(2,1)} %copy-done.4), calls=%async_computation.6 | async-start | bytes 262144 | tf_op jit(solution)/shard_map/slice | solution.py:97
  75.2 15.4 %all-to-all-start.2 = ((bf16[8,76,256]{2,1,0:T(8,128)(2,1)}), bf16[8,76,256]{2,1,0:T(8,128)(2,1)}, u32[]{:S(2)}, u32[]{:S(2)}) async-start(bf16[8,76,256]{2,1,0:T(8,128)(2,1)} %pad_maximum_fusion.3), calls=%async_computation.2 | async-start | bytes 655360 | tf_op jit(solution)/shard_map/all_to_all | solution.py:20
  94.1 11.2 %all-to-all-start.3 = ((bf16[8,32,256]{2,1,0:T(8,128)(2,1)}), bf16[8,32,256]{2,1,0:T(8,128)(2,1)S(1)}, u32[]{:S(2)}, u32[]{:S(2)}) async-start(bf16[8,32,256]{2,1,0:T(8,128)(2,1)} %broadcast_in_dim.29), calls=%async_computation.3 | async-start | bytes 262144 | tf_op jit(solution)/shard_map/all_to_all | solution.py:20
  106.5 33.4 %all-to-all-start.4 = ((bf16[64,32,128]{2,1,0:T(8,128)(2,1)}), bf16[64,32,128]{2,1,0:T(8,128)(2,1)}, u32[]{:S(2)}, u32[]{:S(2)}) async-start(bf16[64,32,128]{2,1,0:T(8,128)(2,1)} %bitcast.93), calls=%async_computation.4 | async-start | bytes 1048576 | tf_op jit(solution)/shard_map/all_to_all | solution.py:20
  122.6 2.2 %copy-start.5 = (f32[3200,128]{0,1:T(8,128)S(1)}, f32[3200,128]{0,1:T(8,128)}, u32[]{:S(2)}) copy-start(f32[3200,128]{0,1:T(8,128)} %fusion.24) | copy-start | bytes 4915204
  139.9 26.0 %all-to-all-start.5 = ((bf16[8,400,256]{2,1,0:T(8,128)(2,1)}), bf16[8,400,256]{2,1,0:T(8,128)(2,1)S(1)}, u32[]{:S(2)}, u32[]{:S(2)}) async-start(bf16[8,400,256]{2,1,0:T(8,128)(2,1)} %bitcast.35), calls=%async_computation.5 | async-start | bytes 3276800 | tf_op jit(solution)/shard_map/all_to_all | solution.py:20
